TPU v7x, 256 devices: a whole 4x4x8 slice. The times are simulated.
256 devices in a mesh: row: 32 (over x, z_hi, core), col: 8 (over z_lo, y).
Axes of the slice: x: 4, y: 4, z: 8 (z_hi: 4, z_lo: 2; z = z_hi * 2 + z_lo), core: 2. Of those that a mesh axis runs over, the one named last changes fastest.
Arguments:
- amplitudes: float32 [32, 8, 1024, 1024], P('row', 'col'), may hold values from -6 to 6
- panels_left: bfloat16 [32, 2, 1024, 1024], P('row', None, 'col'), may hold values from -6 to 6
- panels_right: bfloat16 [8, 2, 1024, 1024], P('col', None, 'row'), may hold values from -6 to 6
- weights_right: bfloat16 [2, 8, 1024, 1024], P(None, 'col', 'row'), may hold values from -0.125 to 0.125
- weights_left: bfloat16 [2, 32, 1024, 1024], P(None, 'row', 'col'), may hold values from -0.125 to 0.125
- energy_left: float32 [32], P('row'), may hold values from -2 to -0.5
- energy_right: float32 [8], P('col'), may hold values from -2 to -0.5
- energy_virtual: float32 [1024], replicated, may hold values from 0.5 to 3
Outputs:
- updated: float32 [32, 8, 1024, 1024], P('row', 'col')
All inputs are finite; a program needn't handle non-finite values.
Results may differ from a plain program's by a relative error of at most 0.0018.
Values may be sent and summed in bfloat16 or wider, within the bound.
A program may use at most 128 MiB of HBM per device.

v0:
```python
import jax
import jax.numpy as jnp
from jax import lax
from jax.sharding import PartitionSpec as P


def combine_blocks(blocks):
    as_float = blocks.astype(jnp.float32)
    return (2.0 * as_float - jnp.swapaxes(as_float, -1, -2)).astype(jnp.bfloat16)


def body(
    amplitudes,
    panels_left,
    panels_right,
    weights_right,
    weights_left,
    energy_left,
    energy_right,
    energy_virtual,
):
    left_slab = panels_left[0]
    right_slab = panels_right[0]
    right_weight_slab = weights_right[:, 0]
    left_weight_slab = weights_left[:, 0]
    left_whole = lax.all_gather(left_slab, "col", axis=1, tiled=True)
    left_mixed = combine_blocks(left_whole)
    mixed_cols = left_mixed
    direct = jnp.einsum(
        "kac,kcb->ab",
        mixed_cols,
        lax.all_gather(right_weight_slab, "row", axis=1, tiled=True),
        preferred_element_type=jnp.float32,
    )
    right_whole = lax.all_gather(right_slab, "row", axis=1, tiled=True)
    right_mixed = combine_blocks(right_whole)
    mixed_cols = right_mixed
    mirror = jnp.einsum(
        "kac,kcb->ab",
        mixed_cols,
        lax.all_gather(left_weight_slab, "col", axis=1, tiled=True),
        preferred_element_type=jnp.float32,
    )
    residual = direct + jnp.transpose(mirror)
    virt_pair = energy_virtual[:, None] + energy_virtual[None, :]
    denominator = energy_left[0] + energy_right[0] - virt_pair
    return (amplitudes[0, 0] + residual / denominator)[None, None]


def solution(mesh):
    placed = (
        P("row", "col", None, None),
        P("row", None, "col", None),
        P("col", None, "row", None),
        P(None, "col", "row", None),
        P(None, "row", "col", None),
        P("row"),
        P("col"),
        P(),
    )
    return jax.shard_map(
        body, mesh=mesh, in_specs=placed, out_specs=P("row", "col", None, None), check_vma=False
    )
```

profile of v0, /device:TPU:1, one launch (start us, length us, event | category | flops | bytes accessed | tf_op | source)
XLA Modules:
  0.0 267.6 jit_solution(162221997629663721)
XLA Ops:
  6.5 0.0 all-gather.9.cloned.1.call-start
  6.5 0.7 all-gather.9.cloned.1.call-update
  7.3 0.0 all-gather.13.cloned.1.call-start
  7.3 0.7 all-gather.13.cloned.1.call-update
  8.0 0.0 all-gather.11.cloned.1.call-start
  8.1 0.7 all-gather.11.cloned.1.call-update
  8.7 0.0 all-gather.15.cloned.1.call-start
  8.8 0.5 all-gather.15.cloned.1.call-update
  10.6 57.3 %all-gather.9.cloned.1.call-done = bf16[1,2,1024,1024]{3,2,1,0:T(8,128)(2,1)} async-done(((bf16[1,2,128,1024]{3,2,1,0:T(8,128)(2,1)}), bf16[1,2,1024,1024]{3,2,1,0:T(8,128)(2,1)}) %all-gather.9.cloned.1.call-update) | async-done | bytes 4194320 | tf_op jit(solution)/shard_map/all_gather | solution.py:26
  68.0 6.5 %bitcast_convert_fusion.1 = f32[2,1024,1024]{2,1,0:T(8,128)} fusion(bf16[1,2,1024,1024]{3,2,1,0:T(8,128)(2,1)} %all-gather.9.cloned.1.call-done), kind=kLoop, calls=%fused_computation.13 | loop fusion | flops 2097152 | bytes 12582912 | tf_op jit(solution)/shard_map/convert_element_type | solution.py:8
  74.4 8.7 %copy.9 = f32[2,1024,1024]{1,2,0:T(8,128)} copy(f32[2,1024,1024]{2,1,0:T(8,128)} %bitcast_convert_fusion.1) | data formatting | bytes 16777216 | tf_op jit(solution)/shard_map/convert_element_type | solution.py:8
  83.1 47.2 %all-gather.13.cloned.1.call-done = bf16[1,2,1024,1024]{3,2,1,0:T(8,128)(2,1)} async-done(((bf16[1,2,32,1024]{3,2,1,0:T(8,128)(2,1)}), bf16[1,2,1024,1024]{3,2,1,0:T(8,128)(2,1)}) %all-gather.13.cloned.1.call-update) | async-done | bytes 4194320 | tf_op jit(solution)/shard_map/all_gather | solution.py:35
  130.2 6.5 %bitcast_convert_fusion = f32[2,1024,1024]{2,1,0:T(8,128)} fusion(bf16[1,2,1024,1024]{3,2,1,0:T(8,128)(2,1)} %all-gather.13.cloned.1.call-done), kind=kLoop, calls=%fused_computation.11 | loop fusion | flops 2097152 | bytes 12582912 | tf_op jit(solution)/shard_map/convert_element_type | solution.py:8
  136.7 8.7 %copy.12 = f32[2,1024,1024]{1,2,0:T(8,128)} copy(f32[2,1024,1024]{2,1,0:T(8,128)} %bitcast_convert_fusion) | data formatting | bytes 16777216 | tf_op jit(solution)/shard_map/convert_element_type | solution.py:8
  145.4 0.0 copy-start
  145.4 45.9 %all-gather.11.cloned.1.call-done = bf16[2,1,1024,1024]{3,2,0,1:T(8,128)(2,1)} async-done(((bf16[2,1,32,1024]{3,2,0,1:T(8,128)(2,1)}), bf16[2,1,1024,1024]{3,2,0,1:T(8,128)(2,1)}) %all-gather.11.cloned.1.call-update) | async-done | bytes 4194320 | tf_op jit(solution)/shard_map/all_gather | solution.py:32
  191.4 12.6 %fusion.2 = f32[1024,1024,1]{1,0,2:T(8,128)} fusion(f32[2,1024,1024]{1,2,0:T(8,128)} %copy.9, bf16[2,1,1024,1024]{3,2,0,1:T(8,128)(2,1)} %all-gather.11.cloned.1.call-done, bf16[1,2,1024,1024]{3,2,1,0:T(8,128)(2,1)} %all-gather.9.cloned.1.call-done), kind=kOutput, calls=%fused_computation.4 | convolution fusion | flops 4303355904 | bytes 20971520 | tf_op jit(solution)/shard_map/kac,kcb->ab/dot_general | solution.py:29
  204.0 41.8 %all-gather.15.cloned.1.call-done = bf16[2,1,1024,1024]{3,2,0,1:T(8,128)(2,1)} async-done(((bf16[2,1,128,1024]{3,2,0,1:T(8,128)(2,1)}), bf16[2,1,1024,1024]{3,2,0,1:T(8,128)(2,1)}) %all-gather.15.cloned.1.call-update) | async-done | bytes 4194320 | tf_op jit(solution)/shard_map/all_gather | solution.py:41
  245.8 0.0 copy-done
  245.8 15.3 %fusion.8 = f32[1,1,1024,1024]{3,2,1,0:T(8,128)} fusion(f32[1024,1024,1]{1,0,2:T(8,128)} %fusion.2, f32[1,1,1024,1024]{3,2,1,0:T(8,128)} %param.8, f32[1024]{0:T(1024)S(1)} %copy-done, f32[]{:T(128)} %bitcast.14, bf16[2,1,1024,1024]{3,2,0,1:T(8,128)(2,1)} %all-gather.15.cloned.1.call-done, f32[2,1024,1024]{1,2,0:T(8,128)} %copy.12, ...), kind=kOutput, calls=%fused_computation.9 | convolution fusion | flops 4308598784 | bytes 29364228 | tf_op jit(solution)/shard_map/kac,kcb->ab/dot_general | solution.py:38
Async XLA Ops:
  6.5 61.4 %all-gather.9.cloned.1.call-start = ((), (), s32[]{:S(2)}) async-start(), calls=%async_computation | async-start | bytes 4718592 | tf_op jit(solution)/shard_map/all_gather | solution.py:26
  7.3 123.0 %all-gather.13.cloned.1.call-start = ((), (), s32[]{:S(2)}) async-start(), calls=%async_computation.2 | async-start | bytes 4325376 | tf_op jit(solution)/shard_map/all_gather | solution.py:35
  8.0 183.4 %all-gather.11.cloned.1.call-start = ((), (), s32[]{:S(2)}) async-start(), calls=%async_computation.1 | async-start | bytes 4325376 | tf_op jit(solution)/shard_map/all_gather | solution.py:32
  8.7 237.0 %all-gather.15.cloned.1.call-start = ((), (), s32[]{:S(2)}) async-start(), calls=%async_computation.3 | async-start | bytes 4718592 | tf_op jit(solution)/shard_map/all_gather | solution.py:41
  145.4 100.3 %copy-start = (f32[1024]{0:T(1024)S(1)}, f32[1024]{0:T(1024)}, u32[]{:S(2)}) copy-start(f32[1024]{0:T(1024)} %param.15) | copy-start | bytes 12292
Sparse Core Ops, SparseCore 0:
  9.1 58.7 all-gather.8
  70.6 59.5 all-gather.12
  132.9 58.4 all-gather.10
  193.0 52.7 all-gather.14
where the time goes:
time: 268 us
  waiting for transfers between devices  195 us (73%)
  matrix products  27.9 us (10%)
  local copies, waits for them, and re-layouts  17.4 us (6%)
  between operations  14.4 us (5%)
  other arithmetic  12.9 us (5%)
    all_gather x1, waiting for transfers between devices, body(): left_whole = lax.all_gather(left_slab, 'col', axis=1, tiled=True)  57.3 us
    all_gather x1, waiting for transfers between devices, body(): right_whole = lax.all_gather(right_slab, 'row', axis=1, tiled=True)  47.2 us
    all_gather x1, waiting for transfers between devices, body(): lax.all_gather(right_weight_slab, 'row', axis=1, tiled=True)  45.9 us
    all_gather x1, waiting for transfers between devices, body(): lax.all_gather(left_weight_slab, 'col', axis=1, tiled=True)  41.8 us
    convert_element_type x2, local copies, waits for them, and re-layouts, combine_blocks(): as_float = blocks.astype(jnp.float32)  17.4 us
    dot_general x1, matrix products, body(): jnp.einsum('kac,kcb->ab', mixed_cols, lax.all_gather(left_weight_slab, 'c...  15.3 us
    convert_element_type x2, other arithmetic, combine_blocks(): as_float = blocks.astype(jnp.float32)  12.9 us
    dot_general x1, matrix products, body(): jnp.einsum('kac,kcb->ab', mixed_cols, lax.all_gather(right_weight_slab, '...  12.6 us
  transfers between devices with their start and end apart: 4, of which 4 were waited for; matrix products, arithmetic and copies ran while one was open for 16% of the time, Pallas kernels for 0%

commit v1 on v0

--- a/solution.py
+++ b/solution.py
@@ -23,7 +23,10 @@
     right_slab = panels_right[0]
     right_weight_slab = weights_right[:, 0]
     left_weight_slab = weights_left[:, 0]
-    left_whole = lax.all_gather(left_slab, "col", axis=1, tiled=True)
+    size = lax.axis_size("col")
+    pieces = jnp.stack([left_slab for _ in range(size)])
+    pieces = lax.all_to_all(pieces, "col", split_axis=0, concat_axis=0)
+    left_whole = jnp.concatenate(pieces, axis=1)
     left_mixed = combine_blocks(left_whole)
     mixed_cols = left_mixed
     direct = jnp.einsum(

time: 268 us -> 220 us (0.82)
  waiting for transfers between devices: 195 us -> 129 us
  other arithmetic: 12.9 us -> 23.2 us
  starting transfers between devices: 0.12 us -> 6.44 us
  local copies, waits for them, and re-layouts: 17.4 us -> 21 us
    all_to_all x0 -> x1, waiting for transfers between devices: none -> 65.3 us  [body(): pieces = lax.all_to_all(pieces, 'col', split_axis=0, concat_axis=0)]
    all_gather x1 -> x0, waiting for transfers between devices: 57.3 us -> none  [body(): left_whole = lax.all_gather(left_slab, 'col', axis=1, tiled=True)]
    all_gather x1, waiting for transfers between devices: 47.2 us -> 0.01 us  [body(): right_whole = lax.all_gather(right_slab, 'row', axis=1, tiled=True)]
    all_gather x1, waiting for transfers between devices: 41.8 us -> 11.3 us  [body(): lax.all_gather(left_weight_slab, 'col', axis=1, tiled=True)]
    convert_element_type x0 -> x1, other arithmetic: none -> 10.2 us  [combine_blocks(): (2.0 * as_float - jnp.swapaxes(as_float, -1, -2)).astype(jnp.bfloat16)]
    all_to_all x0 -> x1, starting transfers between devices: none -> 6.36 us  [body(): pieces = lax.all_to_all(pieces, 'col', split_axis=0, concat_axis=0)]
    all_gather x1, waiting for transfers between devices: 45.9 us -> 49.9 us  [body(): lax.all_gather(right_weight_slab, 'row', axis=1, tiled=True)]
    another operation x0 -> x1, local copies, waits for them, and re-layouts: none -> 3.59 us  [body(): pieces = jnp.stack([left_slab for _ in range(size)])]
  transfers between devices with their start and end apart: 4 -> 4, of which waited for: 4 -> 3; matrix products, arithmetic and copies ran while one was open for 16% -> 26% of each run, Pallas kernels for 0% -> 0%
where the time goes in v1:
time: 220 us; the launch traced here: 219 us
  waiting for transfers between devices  129 us (59%)
  matrix products  25.4 us (12%)
  other arithmetic  23.2 us (11%)
  local copies, waits for them, and re-layouts  21 us (10%)
  between operations  14.4 us (7%)
  starting transfers between devices  6.44 us (3%)
    all_to_all x1, waiting for transfers between devices, body(): pieces = lax.all_to_all(pieces, 'col', split_axis=0, concat_axis=0)  65.3 us
    all_gather x1, waiting for transfers between devices, body(): lax.all_gather(right_weight_slab, 'row', axis=1, tiled=True)  49.9 us
    convert_element_type x2, local copies, waits for them, and re-layouts, combine_blocks(): as_float = blocks.astype(jnp.float32)  17.4 us
    convert_element_type x2, other arithmetic, combine_blocks(): as_float = blocks.astype(jnp.float32)  13 us
    dot_general x1, matrix products, body(): jnp.einsum('kac,kcb->ab', mixed_cols, lax.all_gather(right_weight_slab, '...  12.9 us
    dot_general x1, matrix products, body(): jnp.einsum('kac,kcb->ab', mixed_cols, lax.all_gather(left_weight_slab, 'c...  12.4 us
    all_gather x1, waiting for transfers between devices, body(): lax.all_gather(left_weight_slab, 'col', axis=1, tiled=True)  11.3 us
    convert_element_type x1, other arithmetic, combine_blocks(): (2.0 * as_float - jnp.swapaxes(as_float, -1, -2)).astype(jnp.bfloat16)  10.2 us
  transfers between devices with their start and end apart: 4, of which 3 were waited for; matrix products, arithmetic and copies ran while one was open for 26% of the time, Pallas kernels for 0%

profile of v1, /device:TPU:1, one launch (start us, length us, event | category | flops | bytes accessed | tf_op | source)
XLA Modules:
  0.0 219.0 jit_solution(3987838571597708899)
XLA Ops:
  6.5 0.0 all-gather.9.cloned.1.call-start
  6.5 0.7 all-gather.9.cloned.1.call-update
  7.3 0.0 all-gather.11.cloned.1.call-start
  7.3 0.7 all-gather.11.cloned.1.call-update
  8.0 3.6 %stack.3 = bf16[8,2,128,1024]{3,2,1,0:T(8,128)(2,1)} broadcast(bf16[2,128,1024]{2,1,0:T(8,128)(2,1)} %bitcast.49), dimensions={1,2,3} | broadcast | bytes 4718592 | tf_op jit(solution)/shard_map/stack | solution.py:27
  11.6 6.4 %all-to-all-start = ((bf16[8,2,128,1024]{3,2,1,0:T(8,128)(2,1)}), bf16[8,2,128,1024]{3,2,1,0:T(8,128)(2,1)}, u32[]{:S(2)}, u32[]{:S(2)}) async-start(bf16[8,2,128,1024]{3,2,1,0:T(8,128)(2,1)} %stack.3), calls=%async_computation | async-start | bytes 8388608 | tf_op jit(solution)/shard_map/all_to_all | solution.py:28
  18.0 0.0 all-gather.7.cloned.1.call-start
  18.0 0.7 all-gather.7.cloned.1.call-update
  20.0 65.3 %all-to-all-done = bf16[8,2,128,1024]{3,2,1,0:T(8,128)(2,1)} async-done(((bf16[8,2,128,1024]{3,2,1,0:T(8,128)(2,1)}), bf16[8,2,128,1024]{3,2,1,0:T(8,128)(2,1)}, u32[]{:S(2)}, u32[]{:S(2)}) %all-to-all-start) | async-done | bytes 4194336 | tf_op jit(solution)/shard_map/all_to_all | solution.py:28
  85.3 6.5 %copy_convert_fusion = f32[8,2,128,1024]{3,2,0,1:T(8,128)} fusion(bf16[8,2,128,1024]{3,2,1,0:T(8,128)(2,1)} %all-to-all-done), kind=kLoop, calls=%fused_computation.13 | loop fusion | flops 2097152 | bytes 12582912 | tf_op jit(solution)/shard_map/convert_element_type | solution.py:8
  91.8 8.7 %copy.24 = f32[2,1024,1024]{1,2,0:T(8,128)} copy(f32[2,1024,1024]{2,1,0:T(8,128)} %bitcast.48) | data formatting | bytes 16777216 | tf_op jit(solution)/shard_map/convert_element_type | solution.py:8
  100.4 10.2 %fusion = bf16[2,1024,1024]{1,2,0:T(8,128)(2,1)} fusion(f32[8,2,128,1024]{3,2,0,1:T(8,128)} %copy_convert_fusion, f32[2,1024,1024]{1,2,0:T(8,128)} %copy.24), kind=kLoop, calls=%fused_computation.1 | loop fusion | flops 6291456 | bytes 20971520 | tf_op jit(solution)/shard_map/convert_element_type | solution.py:9
  110.6 0.0 all-gather.9.cloned.1.call-done
  110.6 6.5 %bitcast_convert_fusion = f32[2,1024,1024]{2,1,0:T(8,128)} fusion(bf16[1,2,1024,1024]{3,2,1,0:T(8,128)(2,1)} %all-gather.9.cloned.1.call-done), kind=kLoop, calls=%fused_computation.10 | loop fusion | flops 2097152 | bytes 12582912 | tf_op jit(solution)/shard_map/convert_element_type | solution.py:8
  117.1 8.8 %copy.27 = f32[2,1024,1024]{1,2,0:T(8,128)} copy(f32[2,1024,1024]{2,1,0:T(8,128)} %bitcast_convert_fusion) | data formatting | bytes 16777216 | tf_op jit(solution)/shard_map/convert_element_type | solution.py:8
  125.9 0.0 copy-start
  125.9 11.3 %all-gather.11.cloned.1.call-done = bf16[2,1,1024,1024]{3,2,0,1:T(8,128)(2,1)} async-done(((bf16[2,1,128,1024]{3,2,0,1:T(8,128)(2,1)}), bf16[2,1,1024,1024]{3,2,0,1:T(8,128)(2,1)}) %all-gather.11.cloned.1.call-update) | async-done | bytes 4194320 | tf_op jit(solution)/shard_map/all_gather | solution.py:44
  137.2 12.4 %fusion.2 = f32[1024,1024,1]{0,1,2:T(8,128)} fusion(f32[2,1024,1024]{1,2,0:T(8,128)} %copy.27, bf16[2,1,1024,1024]{3,2,0,1:T(8,128)(2,1)} %all-gather.11.cloned.1.call-done, bf16[1,2,1024,1024]{3,2,1,0:T(8,128)(2,1)} %all-gather.9.cloned.1.call-done), kind=kOutput, calls=%fused_computation.4 | convolution fusion | flops 4303355904 | bytes 20971520 | tf_op jit(solution)/shard_map/kac,kcb->ab/dot_general | solution.py:41
  149.7 49.9 %all-gather.7.cloned.1.call-done = bf16[2,1,1024,1024]{3,2,0,1:T(8,128)(2,1)} async-done(((bf16[2,1,32,1024]{3,2,0,1:T(8,128)(2,1)}), bf16[2,1,1024,1024]{3,2,0,1:T(8,128)(2,1)}) %all-gather.7.cloned.1.call-update) | async-done | bytes 4194320 | tf_op jit(solution)/shard_map/all_gather | solution.py:35
  199.5 0.0 copy-done
  199.5 12.9 %fusion.6 = f32[1,1,1024,1024]{3,2,1,0:T(8,128)} fusion(f32[1024,1024,1]{0,1,2:T(8,128)} %fusion.2, f32[1,1,1024,1024]{3,2,1,0:T(8,128)} %param.8, f32[1024]{0:T(1024)S(1)} %copy-done, f32[]{:T(128)} %bitcast.16, bf16[2,1024,1024]{1,2,0:T(8,128)(2,1)} %fusion, bf16[2,1,1024,1024]{3,2,0,1:T(8,128)(2,1)} %all-gather.7.cloned.1.call-done), kind=kOutput, calls=%fused_computation.8 | convolution fusion | flops 4300210176 | bytes 20975620 | tf_op jit(solution)/shard_map/kac,kcb->ab/dot_general | solution.py:32
Async XLA Ops:
  6.5 104.1 %all-gather.9.cloned.1.call-start = ((), (), s32[]{:S(2)}) async-start(), calls=%async_computation.2 | async-start | bytes 4325376 | tf_op jit(solution)/shard_map/all_gather | solution.py:38
  7.3 130.0 %all-gather.11.cloned.1.call-start = ((), (), s32[]{:S(2)}) async-start(), calls=%async_computation.3 | async-start | bytes 4718592 | tf_op jit(solution)/shard_map/all_gather | solution.py:44
  11.6 73.7 %all-to-all-start = ((bf16[8,2,128,1024]{3,2,1,0:T(8,128)(2,1)}), bf16[8,2,128,1024]{3,2,1,0:T(8,128)(2,1)}, u32[]{:S(2)}, u32[]{:S(2)}) async-start(bf16[8,2,128,1024]{3,2,1,0:T(8,128)(2,1)} %stack.3), calls=%async_computation | async-start | bytes 8388608 | tf_op jit(solution)/shard_map/all_to_all | solution.py:28
  18.0 181.6 %all-gather.7.cloned.1.call-start = ((), (), s32[]{:S(2)}) async-start(), calls=%async_computation.1 | async-start | bytes 4325376 | tf_op jit(solution)/shard_map/all_gather | solution.py:35
  125.9 73.6 %copy-start = (f32[1024]{0:T(1024)S(1)}, f32[1024]{0:T(1024)}, u32[]{:S(2)}) copy-start(f32[1024]{0:T(1024)} %param.15) | copy-start | bytes 12292
Sparse Core Ops, SparseCore 0:
  10.0 73.0 all-gather.8
  84.9 52.2 all-gather.10
  139.9 59.5 all-gather.6
